TPU v7x, 32 devices: a whole 2x2x4 slice. The times are simulated.
32 devices in a mesh: z: 4 (over z), y: 2 (over y), xc: 4 (over x, core).
Axes of the slice: x: 2, y: 2, z: 4, core: 2. Of those that a mesh axis runs over, the one named last changes fastest.
Arguments:
- tokens_x: bfloat16 [262144, 512], P(('z', 'y', 'xc'))
- grad_y: bfloat16 [262144, 512], P(('z', 'y', 'xc'))
- w_one: bfloat16 [512, 2048], replicated
- w_two: bfloat16 [2048, 512], replicated
- w_three: bfloat16 [512, 2048], replicated
- w_four: bfloat16 [2048, 512], replicated
Outputs:
- output 1: float32 [512, 2048], replicated
- output 2: float32 [2048, 512], replicated
- output 3: float32 [512, 2048], replicated
- output 4: float32 [2048, 512], replicated
All inputs are finite; a program needn't handle non-finite values.
Results may differ from a plain program's by a relative error of at most 0.0033.
Values are sent between devices in bfloat16 or wider.
A program may use at most 1 GiB of HBM per device.

v0:
```python
import math
import jax
import jax.numpy as jnp
from jax import lax
from jax.sharding import PartitionSpec as P

GELU_SCALE = math.sqrt(2.0 / math.pi)
GELU_CUBIC = 0.044715


def gelu_value(pre_act):
    return 0.5 * pre_act * (1.0 + jnp.tanh(GELU_SCALE * (pre_act + GELU_CUBIC * pre_act * pre_act * pre_act)))


def gelu_grad(pre_act):
    tanh_val = jnp.tanh(GELU_SCALE * (pre_act + GELU_CUBIC * pre_act * pre_act * pre_act))
    return 0.5 * (1.0 + tanh_val) + 0.5 * pre_act * (1.0 - tanh_val * tanh_val) * GELU_SCALE * (1.0 + 3.0 * GELU_CUBIC * pre_act * pre_act)


def solution(mesh):
    n_dev = math.prod(mesh.shape.values())
    batch_spec = P(("z", "y", "xc"), None)
    whole_spec = P(None, None)

    def reduce_grad(local_grad):
        reduced = lax.psum_scatter(local_grad, "xc", scatter_dimension=0, tiled=True)
        reduced = lax.psum_scatter(reduced, "y", scatter_dimension=0, tiled=True)
        reduced = lax.psum(reduced, "z")
        reduced = lax.all_gather(reduced, "y", axis=0, tiled=True)
        reduced = lax.all_gather(reduced, "xc", axis=0, tiled=True)
        return reduced / n_dev

    def device_step(x_loc, g_loc, w_one, w_two, w_three, w_four):
        a_one = jnp.dot(x_loc, w_one, preferred_element_type=jnp.float32).astype(jnp.bfloat16)
        h_one = gelu_value(a_one.astype(jnp.float32)).astype(jnp.bfloat16)
        h_two = (jnp.dot(h_one, w_two, preferred_element_type=jnp.float32) + x_loc.astype(jnp.float32)).astype(jnp.bfloat16)
        a_three = jnp.dot(h_two, w_three, preferred_element_type=jnp.float32).astype(jnp.bfloat16)
        h_three = gelu_value(a_three.astype(jnp.float32)).astype(jnp.bfloat16)
        grad_w4 = reduce_grad(jnp.einsum("nf,nd->fd", h_three, g_loc, preferred_element_type=jnp.float32))
        d_a3 = (jnp.einsum("nd,fd->nf", g_loc, w_four, preferred_element_type=jnp.float32) * gelu_grad(a_three.astype(jnp.float32))).astype(jnp.bfloat16)
        grad_w3 = reduce_grad(jnp.einsum("nd,nf->df", h_two, d_a3, preferred_element_type=jnp.float32))
        d_h2 = (jnp.einsum("nf,df->nd", d_a3, w_three, preferred_element_type=jnp.float32) + g_loc.astype(jnp.float32)).astype(jnp.bfloat16)
        grad_w2 = reduce_grad(jnp.einsum("nf,nd->fd", h_one, d_h2, preferred_element_type=jnp.float32))
        d_a1 = (jnp.einsum("nd,fd->nf", d_h2, w_two, preferred_element_type=jnp.float32) * gelu_grad(a_one.astype(jnp.float32))).astype(jnp.bfloat16)
        grad_w1 = reduce_grad(jnp.einsum("nd,nf->df", x_loc, d_a1, preferred_element_type=jnp.float32))
        return grad_w1, grad_w2, grad_w3, grad_w4

    return jax.shard_map(
        device_step,
        mesh=mesh,
        in_specs=(batch_spec, batch_spec, whole_spec, whole_spec, whole_spec, whole_spec),
        out_specs=(whole_spec, whole_spec, whole_spec, whole_spec),
        check_vma=False,
    )
```

profile of v0, /device:TPU:0, one launch (start us, length us, event | category | flops | bytes accessed | tf_op | source)
XLA Modules:
  0.0 874.9 jit_solution(17168219227449171776)
XLA Ops:
  7.2 24.7 %convolution_convert_fusion.1 = bf16[8192,2048]{1,0:T(8,128)(2,1)} fusion(bf16[8192,512]{1,0:T(8,128)(2,1)} %param.6, bf16[512,2048]{1,0:T(8,128)(2,1)} %param.8), kind=kOutput, calls=%fused_computation.38 | convolution fusion | flops 17196646400 | bytes 44040192 | tf_op jit(solution)/shard_map/dot_general | solution.py:34
  31.9 33.6 %add_convert_fusion.1 = bf16[8192,512]{1,0:T(8,128)(2,1)} fusion(bf16[8192,512]{1,0:T(8,128)(2,1)} %param.6, bf16[2048,512]{1,0:T(8,128)(2,1)} %param.9, bf16[8192,2048]{1,0:T(8,128)(2,1)} %convolution_convert_fusion.1), kind=kOutput, calls=%fused_computation.41 | convolution fusion | flops 17360224256 | bytes 52428800 | tf_op jit(solution)/shard_map/dot_general | solution.py:36
  65.5 24.9 %convolution_convert_fusion = bf16[8192,2048]{1,0:T(8,128)(2,1)} fusion(bf16[8192,512]{1,0:T(8,128)(2,1)} %add_convert_fusion.1, bf16[512,2048]{1,0:T(8,128)(2,1)S(1)} %copy-done), kind=kOutput, calls=%fused_computation.37 | convolution fusion | flops 17196646400 | bytes 44040192 | tf_op jit(solution)/shard_map/dot_general | solution.py:37
  90.4 57.9 %fusion.8 = bf16[8192,2048]{1,0:T(8,128)(2,1)} fusion(bf16[8192,2048]{1,0:T(8,128)(2,1)} %convolution_convert_fusion, bf16[8192,512]{1,0:T(8,128)(2,1)} %param.7, bf16[2048,512]{1,0:T(8,128)(2,1)} %param.11), kind=kOutput, calls=%fused_computation.22 | convolution fusion | flops 17515413504 | bytes 77594624 | tf_op jit(solution)/shard_map/nd,fd->nf/dot_general | solution.py:40
  148.3 22.4 %fusion.38 = f32[512,2048]{1,0:T(8,128)} fusion(bf16[8192,512]{1,0:T(8,128)(2,1)S(1)} %copy-done.4, bf16[8192,2048]{1,0:T(8,128)(2,1)} %fusion.8), kind=kOutput, calls=%fused_computation.57 | convolution fusion | flops 17179869184 | bytes 46137344 | tf_op jit(solution)/shard_map/nd,nf->df/dot_general | solution.py:41
  170.7 0.0 reduce-scatter.13.cloned.1.call-start
  170.8 25.0 %add_convert_fusion = bf16[8192,512]{1,0:T(8,128)(2,1)} fusion(bf16[8192,512]{1,0:T(8,128)(2,1)} %param.7, bf16[8192,2048]{1,0:T(8,128)(2,1)} %fusion.8, bf16[512,2048]{1,0:T(8,128)(2,1)S(1)} %copy-done), kind=kOutput, calls=%fused_computation.40 | convolution fusion | flops 17192452096 | bytes 52428800 | tf_op jit(solution)/shard_map/nf,df->nd/dot_general | solution.py:42
  195.8 56.9 %fusion.15.clone.6 = bf16[8192,2048]{1,0:T(8,128)(2,1)} fusion(bf16[8192,2048]{1,0:T(8,128)(2,1)} %convolution_convert_fusion.1, bf16[8192,512]{1,0:T(8,128)(2,1)} %add_convert_fusion, bf16[2048,512]{1,0:T(8,128)(2,1)S(1)} %copy-done.3), kind=kOutput, calls=%fused_computation.29.clone.clone.clone.clone.clone.1 | convolution fusion | flops 17515413504 | bytes 77594624 | tf_op jit(solution)/shard_map/nd,fd->nf/dot_general | solution.py:44
  252.7 22.4 %fusion.25 = f32[512,2048]{0,1:T(8,128)} fusion(bf16[8192,512]{1,0:T(8,128)(2,1)S(1)} %copy-done.2, bf16[8192,2048]{1,0:T(8,128)(2,1)} %fusion.15.clone.6), kind=kOutput, calls=%fused_computation.42 | convolution fusion | flops 17179869184 | bytes 46137344 | tf_op jit(solution)/shard_map/nd,nf->df/dot_general | solution.py:45
  275.1 0.0 reduce-scatter.21.cloned.1.call-start
  275.2 35.7 %fusion.22 = f32[2048,512]{1,0:T(8,128)} fusion(bf16[8192,512]{1,0:T(8,128)(2,1)} %param.7, bf16[8192,2048]{1,0:T(8,128)(2,1)} %convolution_convert_fusion), kind=kOutput, calls=%fused_computation.36 | convolution fusion | flops 17347641344 | bytes 46137344 | tf_op jit(solution)/shard_map/nf,nd->fd/dot_general | solution.py:39
  310.9 0.0 reduce-scatter.15.cloned.1.call-start
  311.0 35.9 %fusion.35 = f32[2048,512]{1,0:T(8,128)} fusion(bf16[8192,512]{1,0:T(8,128)(2,1)} %add_convert_fusion, bf16[8192,2048]{1,0:T(8,128)(2,1)} %convolution_convert_fusion.1), kind=kOutput, calls=%fused_computation.56 | convolution fusion | flops 17347641344 | bytes 46137344 | tf_op jit(solution)/shard_map/nf,nd->fd/dot_general | solution.py:43
  346.8 0.0 reduce-scatter.27.cloned.1.call-start
  346.9 0.5 reduce-scatter.27.cloned.1.call-update
  347.4 0.0 reduce-scatter.25.cloned.1.call-start
  347.5 2.5 copy.16
  350.0 0.0 reduce-scatter.23.cloned.1.call-start
  350.1 18.7 %reduce-scatter.21.cloned.1.call-done = f32[512,512]{1,0:T(8,128)} async-done(((f32[2048,512]{1,0:T(8,128)}), f32[512,512]{1,0:T(8,128)}) %reduce-scatter.21.cloned.1.call-update) | async-done | bytes 1048592 | tf_op jit(solution)/shard_map/reduce_scatter | solution.py:26
  368.9 46.8 %reduce-scatter.15.cloned.1.call-done = f32[512,512]{1,0:T(8,128)} async-done(((f32[2048,512]{1,0:T(8,128)}), f32[512,512]{1,0:T(8,128)}) %reduce-scatter.15.cloned.1.call-update) | async-done | bytes 1048592 | tf_op jit(solution)/shard_map/reduce_scatter | solution.py:26
  415.7 0.0 all-reduce.3.cloned.1.call-start
  415.7 22.3 %reduce-scatter.27.cloned.1.call-done = f32[64,2048]{1,0:T(8,128)} async-done(((f32[128,2048]{1,0:T(8,128)}), f32[64,2048]{1,0:T(8,128)}) %reduce-scatter.27.cloned.1.call-update) | async-done | bytes 524304
  438.1 2.4 copy.19
  440.4 20.6 %reduce-scatter.25.cloned.1.call-done = f32[64,2048]{1,0:T(8,128)} async-done(((f32[128,2048]{1,0:T(8,128)}), f32[64,2048]{1,0:T(8,128)}) %reduce-scatter.25.cloned.1.call-update) | async-done | bytes 524304
  461.1 2.4 copy.17
  463.4 20.2 %reduce-scatter.23.cloned.1.call-done = f32[256,512]{1,0:T(8,128)} async-done(((f32[512,512]{1,0:T(8,128)}), f32[256,512]{1,0:T(8,128)}) %reduce-scatter.23.cloned.1.call-update) | async-done | bytes 524304 | tf_op jit(solution)/shard_map/reduce_scatter | solution.py:27
  483.6 22.6 %reduce-scatter.17.cloned.1.call-done = f32[256,512]{1,0:T(8,128)} async-done(((f32[512,512]{1,0:T(8,128)}), f32[256,512]{1,0:T(8,128)}) %reduce-scatter.17.cloned.1.call-update) | async-done | bytes 524304 | tf_op jit(solution)/shard_map/reduce_scatter | solution.py:27
  506.2 0.0 all-gather.9.cloned.1.call-start
  506.3 123.0 %all-reduce.3.cloned.1.call-done = (f32[64,2048]{0,1:T(8,128)}, f32[256,512]{1,0:T(8,128)}, f32[64,2048]{0,1:T(8,128)}, f32[256,512]{1,0:T(8,128)}) async-done(((f32[64,2048]{0,1:T(8,128)}, f32[256,512]{1,0:T(8,128)}, f32[64,2048]{0,1:T(8,128)}, f32[256,512]{1,0:T(8,128)}), (f32[64,2048]{0,1:T(8,128)}, f32[256,512]{1,0:T(8,128)}, f32[64,2048]{0,1:T(8,128)}, ...) | async-done | bytes 2097168 | tf_op jit(solution)/shard_map/psum | solution.py:28
  629.3 2.3 copy.13
  631.7 0.0 all-gather.13.cloned.1.call-start
  631.7 0.7 all-gather.13.cloned.1.call-update
  632.5 0.5 all-gather.21.cloned.1.call-update
  633.0 0.0 all-gather.17.cloned.1.call-start
  633.0 2.3 copy.15
  635.4 0.0 all-gather.11.cloned.1.call-start
  635.5 16.6 %all-gather.9.cloned.1.call-done = f32[128,2048]{1,0:T(8,128)} async-done(((f32[64,2048]{1,0:T(8,128)}), f32[128,2048]{1,0:T(8,128)}) %all-gather.9.cloned.1.call-update) | async-done | bytes 1048592 | tf_op jit(solution)/shard_map/all_gather | solution.py:29
  652.1 22.5 %all-gather.13.cloned.1.call-done = f32[512,512]{1,0:T(8,128)} async-done(((f32[256,512]{1,0:T(8,128)}), f32[512,512]{1,0:T(8,128)}) %all-gather.13.cloned.1.call-update) | async-done | bytes 1048592 | tf_op jit(solution)/shard_map/all_gather | solution.py:29
  674.7 22.4 %all-gather.21.cloned.1.call-done = f32[512,512]{1,0:T(8,128)} async-done(((f32[256,512]{1,0:T(8,128)}), f32[512,512]{1,0:T(8,128)}) %all-gather.21.cloned.1.call-update) | async-done | bytes 1048592 | tf_op jit(solution)/shard_map/all_gather | solution.py:29
  697.2 23.1 %all-gather.17.cloned.1.call-done = f32[128,2048]{1,0:T(8,128)} async-done(((f32[64,2048]{1,0:T(8,128)}), f32[128,2048]{1,0:T(8,128)}) %all-gather.17.cloned.1.call-update) | async-done | bytes 1048592 | tf_op jit(solution)/shard_map/all_gather | solution.py:29
  720.3 35.7 %all-gather.11.cloned.1.call-done = f32[512,2048]{1,0:T(8,128)} async-done(((f32[128,2048]{1,0:T(8,128)}), f32[512,2048]{1,0:T(8,128)}) %all-gather.11.cloned.1.call-update) | async-done | bytes 4194320 | tf_op jit(solution)/shard_map/all_gather | solution.py:30
  756.0 4.8 broadcast_multiply_fusion.3
  760.8 30.9 %all-gather.15.cloned.1.call-done = f32[2048,512]{1,0:T(8,128)} async-done(((f32[512,512]{1,0:T(8,128)}), f32[2048,512]{1,0:T(8,128)}) %all-gather.15.cloned.1.call-update) | async-done | bytes 4194320 | tf_op jit(solution)/shard_map/all_gather | solution.py:30
  791.7 4.7 broadcast_multiply_fusion.1
  796.4 31.0 %all-gather.23.cloned.1.call-done = f32[2048,512]{1,0:T(8,128)} async-done(((f32[512,512]{1,0:T(8,128)}), f32[2048,512]{1,0:T(8,128)}) %all-gather.23.cloned.1.call-update) | async-done | bytes 4194320 | tf_op jit(solution)/shard_map/all_gather | solution.py:30
  827.5 4.7 broadcast_multiply_fusion
  832.2 31.0 %all-gather.19.cloned.1.call-done = f32[512,2048]{1,0:T(8,128)} async-done(((f32[128,2048]{1,0:T(8,128)}), f32[512,2048]{1,0:T(8,128)}) %all-gather.19.cloned.1.call-update) | async-done | bytes 4194320 | tf_op jit(solution)/shard_map/all_gather | solution.py:30
  863.2 4.8 broadcast_multiply_fusion.2
  (32 shorter events, 0.5 us)
Async XLA Ops:
  7.2 58.4 %copy-start = (bf16[512,2048]{1,0:T(8,128)(2,1)S(1)}, bf16[512,2048]{1,0:T(8,128)(2,1)}, u32[]{:S(2)}) copy-start(bf16[512,2048]{1,0:T(8,128)(2,1)} %param.10) | copy-start | bytes 6291460
  7.2 339.7 %reduce-scatter.19.cloned.1.call-start = ((), (), s32[]{:S(2)}) async-start(), calls=%async_computation.15 | async-start | bytes 5242880 | tf_op jit(solution)/shard_map/reduce_scatter | solution.py:26
  90.4 57.9 %copy-start.4 = (bf16[8192,512]{1,0:T(8,128)(2,1)S(1)}, bf16[8192,512]{1,0:T(8,128)(2,1)}, u32[]{:S(2)}) copy-start(bf16[8192,512]{1,0:T(8,128)(2,1)} %add_convert_fusion.1) | copy-start | bytes 25165828
  170.7 176.8 %reduce-scatter.13.cloned.1.call-start = ((), (), s32[]{:S(2)}) async-start(), calls=%async_computation.8 | async-start | bytes 5242880 | tf_op jit(solution)/shard_map/reduce_scatter | solution.py:26
  170.8 25.0 %copy-start.3 = (bf16[2048,512]{1,0:T(8,128)(2,1)S(1)}, bf16[2048,512]{1,0:T(8,128)(2,1)}, u32[]{:S(2)}) copy-start(bf16[2048,512]{1,0:T(8,128)(2,1)} %param.9) | copy-start | bytes 6291460
  195.8 56.9 %copy-start.2 = (bf16[8192,512]{1,0:T(8,128)(2,1)S(1)}, bf16[8192,512]{1,0:T(8,128)(2,1)}, u32[]{:S(2)}) copy-start(bf16[8192,512]{1,0:T(8,128)(2,1)} %param.6) | copy-start | bytes 25165828
  275.1 93.7 %reduce-scatter.21.cloned.1.call-start = ((), (), s32[]{:S(2)}) async-start(), calls=%async_computation.18 | async-start | bytes 5242880 | tf_op jit(solution)/shard_map/reduce_scatter | solution.py:26
  310.9 104.8 %reduce-scatter.15.cloned.1.call-start = ((), (), s32[]{:S(2)}) async-start(), calls=%async_computation.11 | async-start | bytes 5242880 | tf_op jit(solution)/shard_map/reduce_scatter | solution.py:26
  310.9 557.0 %copy-start.1 = (bf16[512,2048]{1,0:T(8,128)(2,1)S(1)}, bf16[512,2048]{1,0:T(8,128)(2,1)}, u32[]{:S(2)}) copy-start(bf16[512,2048]{1,0:T(8,128)(2,1)} %param.10) | copy-start | bytes 6291460
  346.8 91.3 %reduce-scatter.27.cloned.1.call-start = ((), (), s32[]{:S(2)}) async-start(), calls=%async_computation.23 | async-start | bytes 1572864
  347.4 113.7 %reduce-scatter.25.cloned.1.call-start = ((), (), s32[]{:S(2)}) async-start(), calls=%async_computation.22 | async-start | bytes 1572864
  350.0 133.6 %reduce-scatter.23.cloned.1.call-start = ((), (), s32[]{:S(2)}) async-start(), calls=%async_computation.19 | async-start | bytes 1572864 | tf_op jit(solution)/shard_map/reduce_scatter | solution.py:27
  368.9 137.3 %reduce-scatter.17.cloned.1.call-start = ((), (), s32[]{:S(2)}) async-start(), calls=%async_computation.12 | async-start | bytes 1572864 | tf_op jit(solution)/shard_map/reduce_scatter | solution.py:27
  415.7 213.6 %all-reduce.3.cloned.1.call-start = ((), (), s32[]{:S(2)}) async-start(), calls=%async_computation.24 | async-start | bytes 6291456 | tf_op jit(solution)/shard_map/psum | solution.py:28
  506.2 145.8 %all-gather.9.cloned.1.call-start = ((), (), s32[]{:S(2)}) async-start(), calls=%async_computation.9 | async-start | bytes 1572864 | tf_op jit(solution)/shard_map/all_gather | solution.py:29
  631.7 42.9 %all-gather.13.cloned.1.call-start = ((), (), s32[]{:S(2)}) async-start(), calls=%async_computation.13 | async-start | bytes 1572864 | tf_op jit(solution)/shard_map/all_gather | solution.py:29
  632.4 64.7 %all-gather.21.cloned.1.call-start = ((), (), s32[]{:S(2)}) async-start(), calls=%async_computation.20 | async-start | bytes 1572864 | tf_op jit(solution)/shard_map/all_gather | solution.py:29
  633.0 87.3 %all-gather.17.cloned.1.call-start = ((), (), s32[]{:S(2)}) async-start(), calls=%async_computation.16 | async-start | bytes 1572864 | tf_op jit(solution)/shard_map/all_gather | solution.py:29
  635.4 120.6 %all-gather.11.cloned.1.call-start = ((), (), s32[]{:S(2)}) async-start(), calls=%async_computation.10 | async-start | bytes 5242880 | tf_op jit(solution)/shard_map/all_gather | solution.py:30
  652.0 139.7 %all-gather.15.cloned.1.call-start = ((), (), s32[]{:S(2)}) async-start(), calls=%async_computation.14 | async-start | bytes 5242880 | tf_op jit(solution)/shard_map/all_gather | solution.py:30
  674.6 152.8 %all-gather.23.cloned.1.call-start = ((), (), s32[]{:S(2)}) async-start(), calls=%async_computation.21 | async-start | bytes 5242880 | tf_op jit(solution)/shard_map/all_gather | solution.py:30
  697.1 166.1 %all-gather.19.cloned.1.call-start = ((), (), s32[]{:S(2)}) async-start(), calls=%async_computation.17 | async-start | bytes 5242880 | tf_op jit(solution)/shard_map/all_gather | solution.py:30
Sparse Core Ops, SparseCore 0:
  170.9 46.5 reduce-scatter.18
  275.2 46.5 reduce-scatter.12
  325.0 43.8 reduce-scatter.20
  371.8 43.8 reduce-scatter.14
  417.8 20.2 reduce-scatter.26
  440.8 20.2 reduce-scatter.24
  463.3 20.2 reduce-scatter.22
  485.9 20.2 reduce-scatter.16
  509.4 119.8 all-reduce.2
  631.8 20.1 all-gather.8
  653.6 21.0 all-gather.12
  676.0 21.0 all-gather.20
  699.2 21.0 all-gather.16
  721.7 34.2 all-gather.10
  757.4 34.2 all-gather.14
  793.1 34.2 all-gather.22
  828.9 34.2 all-gather.18
where the time goes:
time: 880 us; the launch traced here: 875 us
  waiting for transfers between devices  490 us (56%)
  matrix products  339 us (39%)
  other arithmetic  19 us (2%)
  between operations  14.5 us (2%)
  local copies, waits for them, and re-layouts  11.9 us (1%)
    all_gather x4, waiting for transfers between devices, reduce_grad(): reduced = lax.all_gather(reduced, 'xc', axis=0, tiled=True)  129 us
    psum x1, waiting for transfers between devices, reduce_grad(): reduced = lax.psum(reduced, 'z')  123 us
    all_gather x4, waiting for transfers between devices, reduce_grad(): reduced = lax.all_gather(reduced, 'y', axis=0, tiled=True)  84.6 us
    reduce_scatter x4, waiting for transfers between devices, reduce_grad(): lax.psum_scatter(local_grad, 'xc', scatter_dimension=0, tiled=True)  65.5 us
    dot_general x1, matrix products, device_step(): jnp.einsum('nd,fd->nf', g_loc, w_four, preferred_element_type=jnp.float32)  57.9 us
    dot_general x1, matrix products, device_step(): jnp.einsum('nd,fd->nf', d_h2, w_two, preferred_element_type=jnp.float32)  56.9 us
    unnamed x19, waiting for transfers between devices  44.9 us
    reduce_scatter x2, waiting for transfers between devices, reduce_grad(): reduced = lax.psum_scatter(reduced, 'y', scatter_dimension=0, tiled=True)  42.8 us
  transfers between devices with their start and end apart: 17, of which 15 were waited for; matrix products, arithmetic and copies ran while one was open for 23% of the time, Pallas kernels for 0%

commit v1 on v0

v1 whole, which is shorter than its diff:
```python
import functools
import math
import jax
import jax.numpy as jnp
from jax import lax
from jax.experimental import pallas as pl
from jax.experimental.pallas import tpu as pltpu
from jax.sharding import PartitionSpec as P

C0 = math.sqrt(2.0 / math.pi)
K0 = 0.044715
F32 = jnp.float32
BF16 = jnp.bfloat16
MESH = pl.DeviceIdType.MESH
VMEM_LIMIT = 67_000_000

NCH = 4
NRB = 8
UNITS = 2 * NCH
SLOTS = 4
SUBS = 2

OFF = dict(d=0, s1=2, s2=6, z=9, zg=14, s2g=19, s1g=22, dg=26, end=29)


def nn(a, b):
    return jnp.dot(a, b, preferred_element_type=F32)


def nt(a, b):
    return lax.dot_general(a, b, (((1,), (1,)), ((), ())), preferred_element_type=F32)


def tn(a, b):
    return lax.dot_general(a, b, (((0,), (0,)), ((), ())), preferred_element_type=F32)


def gelu_only(a):
    kq = (K0 * a) * a
    t = jnp.tanh((C0 * a) * (1.0 + kq))
    return a * (0.5 * t + 0.5)


def gelu_both(a):
    kq = (K0 * a) * a
    t = jnp.tanh((C0 * a) * (1.0 + kq))
    s = 0.5 * t + 0.5
    h = a * s
    grad = s + (h * (C0 - C0 * t)) * (1.0 + 3.0 * kq)
    return h, grad


def fwd_kernel(x_ref, w1_ref, w2_ref, a1_ref, h2_ref):
    ffc = w1_ref.shape[1] // NCH
    x = x_ref[...]
    acc = x.astype(F32)
    for c in range(NCH):
        cols = slice(c * ffc, (c + 1) * ffc)
        a1 = nn(x, w1_ref[:, cols]).astype(BF16)
        a1_ref[:, cols] = a1
        h1 = gelu_only(a1.astype(F32)).astype(BF16)
        acc += nn(h1, w2_ref[cols, :])
    h2_ref[...] = acc.astype(BF16)


def grad_kernel(
    x_hbm, g_hbm, h2_hbm, a1_hbm, w2_hbm, w3_hbm, w4_hbm, o_hbm,
    h2, gx, dh, w2, w3, w4, a1b, pb, q, r1, r2, rz,
    wsem, hsem, gsem, xsem, asem, lsem, ssem, rsem, csem,
):
    d = h2.shape[1]
    rows = h2.shape[0] // NRB
    ffc = w3.shape[1] // NCH
    half, col, s1n, s2n, zn = d // 2, d // 4, d // 8, d // 16, d // 64

    xc, y, z = lax.axis_index("xc"), lax.axis_index("y"), lax.axis_index("z")
    x, core = lax.div(xc, 2), lax.rem(xc, 2)
    to_core = {"xc": xc + 1 - 2 * core}
    to_x = {"xc": core + 2 * (1 - x)}
    to_y = {"y": 1 - y}
    to_z = [{"z": lax.rem(z + j, 4)} for j in (1, 2, 3)]
    peers = [to_core, to_x, to_y] + to_z

    def al(v, m):
        return pl.multiple_of(v, m)

    def block(i):
        return pl.ds(al(i * rows, rows), rows)

    w_copies = [
        pltpu.make_async_copy(src, dst, wsem.at[i])
        for i, (src, dst) in enumerate(((w3_hbm, w3), (w4_hbm, w4), (w2_hbm, w2)))
    ]

    def h_copy(i):
        return pltpu.make_async_copy(h2_hbm.at[block(i)], h2.at[block(i)], hsem.at[i])

    def g_copy(i):
        return pltpu.make_async_copy(g_hbm.at[block(i)], gx.at[block(i)], gsem.at[i])

    def x_copy(i):
        return pltpu.make_async_copy(x_hbm.at[block(i)], gx.at[block(i)], xsem.at[i])

    def a_copy(i):
        c, r = lax.div(i, NRB), lax.rem(i, NRB)
        slot = lax.rem(i, 2)
        return pltpu.make_async_copy(
            a1_hbm.at[block(r), pl.ds(al(c * ffc, ffc), ffc)], a1b.at[slot], asem.at[slot]
        )

    w_copies[0].start()
    h_copy(0).start()
    w_copies[1].start()
    g_copy(0).start()
    for i in range(1, NRB):
        h_copy(i).start()
        g_copy(i).start()
    w_copies[2].start()
    a_copy(jnp.int32(0)).start()

    barrier = pltpu.get_barrier_semaphore()
    for peer in peers:
        pl.semaphore_signal(barrier, inc=1, device_id=peer, device_id_type=MESH)
    pl.semaphore_wait(barrier, len(peers))

    xa, yb = x * s1n, col + y * s1n
    xya, yxb = xa + y * s2n, yb + x * s2n

    def remote(src, dst, k, i, peer):
        return pltpu.make_async_remote_copy(
            src_ref=src, dst_ref=dst, send_sem=ssem.at[k, i], recv_sem=rsem.at[k, i],
            device_id=peer, device_id_type=MESH,
        )

    def c_d(k):
        return [remote(
            pb.at[lax.rem(k, 2), :, pl.ds(al((1 - core) * half, half), half), :],
            q.at[lax.rem(k, SLOTS)], k, 0, to_core)]

    def q_at(k, start, size):
        return q.at[lax.rem(k, SLOTS), :, pl.ds(al(start, zn), size), :]

    def o_at(k, start, size):
        return o_hbm.at[k, :, pl.ds(al(core * half + start, zn), size), :]

    def c_s1(k):
        sl = lax.rem(k, SLOTS)
        return [
            remote(q_at(k, (1 - x) * s1n, s1n), r1.at[sl, 0], k, 1, to_x),
            remote(q_at(k, col + (1 - y) * s1n, s1n), r1.at[sl, 1], k, 2, to_y),
        ]

    def c_s2(k):
        sl = lax.rem(k, SLOTS)
        return [
            remote(q_at(k, xa + (1 - y) * s2n, s2n), r2.at[sl, 0], k, 3, to_y),
            remote(q_at(k, yb + (1 - x) * s2n, s2n), r2.at[sl, 1], k, 4, to_x),
        ]

    def c_z(k):
        sl = lax.rem(k, SLOTS)
        out = []
        for j in range(3):
            zz = lax.rem(z + j + 1, 4) * zn
            out.append(remote(q_at(k, xya + zz, zn), rz.at[sl, j, 0], k, 5 + 2 * j, to_z[j]))
            out.append(remote(q_at(k, yxb + zz, zn), rz.at[sl, j, 1], k, 6 + 2 * j, to_z[j]))
        return out

    def c_zg(k):
        out = []
        for j in range(3):
            for n, base in enumerate((xya, yxb)):
                at = base + z * zn
                out.append(remote(q_at(k, at, zn), o_at(k, at, zn), k, 11 + 2 * j + n, to_z[j]))
        return out

    def c_local(k):
        return [
            pltpu.make_async_copy(q_at(k, base + z * zn, zn), o_at(k, base + z * zn, zn), lsem.at[k, n])
            for n, base in enumerate((xya, yxb))
        ]

    def c_s2g(k):
        return [
            remote(o_at(k, xya, s2n), o_at(k, xya, s2n), k, 17, to_y),
            remote(o_at(k, yxb, s2n), o_at(k, yxb, s2n), k, 18, to_x),
        ]

    def c_s1g(k):
        return [
            remote(o_at(k, xa, s1n), o_at(k, xa, s1n), k, 19, to_x),
            remote(o_at(k, yb, s1n), o_at(k, yb, s1n), k, 20, to_y),
        ]

    def c_dg(k):
        return [remote(o_at(k, 0, half), o_at(k, 0, half), k, 21, to_core)]

    def start(copies):
        for copy in copies:
            copy.start()

    def wait(copies):
        for copy in copies:
            copy.wait()

    def q_add(k, at, size, value):
        sl = lax.rem(k, SLOTS)
        ds = pl.ds(al(at, zn), size)
        q[sl, :, ds, :] = q[sl, :, ds, :] + value

    def stage(g, name, action):
        t = g - OFF[name] - NRB
        k = lax.div(t, NRB)

        @pl.when((t >= 0) & (lax.rem(t, NRB) == 0) & (k < UNITS))
        def _():
            action(k)

    def do_d(k):
        @pl.when(k >= SLOTS)
        def _():
            pl.semaphore_wait(csem.at[lax.rem(k, SLOTS)], len(peers))
        start(c_d(k))

    def do_s1(k):
        wait(c_d(k))
        sl = lax.rem(k, SLOTS)
        q[sl] = q[sl] + pb[lax.rem(k, 2), :, pl.ds(al(core * half, half), half), :]
        start(c_s1(k))

    def do_s2(k):
        wait(c_s1(k))
        sl = lax.rem(k, SLOTS)
        q_add(k, xa, s1n, r1[sl, 0])
        q_add(k, yb, s1n, r1[sl, 1])
        start(c_s2(k))

    def do_z(k):
        wait(c_s2(k))
        sl = lax.rem(k, SLOTS)
        q_add(k, xya, s2n, r2[sl, 0])
        q_add(k, yxb, s2n, r2[sl, 1])
        start(c_z(k))

    def do_zg(k):
        wait(c_z(k))
        sl = lax.rem(k, SLOTS)
        for n, base in enumerate((xya, yxb)):
            ds = pl.ds(al(base + z * zn, zn), zn)
            total = (q[sl, :, ds, :] + rz[sl, 0, n]) + (rz[sl, 1, n] + rz[sl, 2, n])
            q[sl, :, ds, :] = total * (1.0 / 32.0)
        start(c_zg(k))
        start(c_local(k))

    def do_s2g(k):
        wait(c_zg(k))
        wait(c_local(k))

        @pl.when(k < UNITS - SLOTS)
        def _():
            for peer in peers:
                pl.semaphore_signal(csem.at[lax.rem(k, SLOTS)], inc=1, device_id=peer, device_id_type=MESH)
        start(c_s2g(k))

    def do_s1g(k):
        wait(c_s2g(k))
        start(c_s1g(k))

    def do_dg(k):
        wait(c_s1g(k))
        start(c_dg(k))

    def do_end(k):
        wait(c_dg(k))

    def comm(g):
        stage(g, "d", do_d)
        stage(g, "end", do_end)
        stage(g, "dg", do_dg)
        stage(g, "s1g", do_s1g)
        stage(g, "s2g", do_s2g)
        stage(g, "zg", do_zg)
        stage(g, "z", do_z)
        stage(g, "s2", do_s2)
        stage(g, "s1", do_s1)

    sub = rows // SUBS

    def first_step(g, carry):
        c, r = lax.div(g, NRB), lax.rem(g, NRB)
        par = lax.rem(c, 2)
        comm(g)

        @pl.when(g == 0)
        def _():
            w_copies[0].wait()
            w_copies[1].wait()

        @pl.when(c == 0)
        def _():
            h_copy(r).wait()
            g_copy(r).wait()

        @pl.when(r == 0)
        def _():
            pb[par] = jnp.zeros_like(pb[par])

        cols = pl.ds(al(c * ffc, ffc), ffc)
        wc3 = w3[:, cols]
        wc4 = w4[cols, :]
        for i in range(SUBS):
            ds = pl.ds(al(r * rows + i * sub, sub), sub)
            h2r, gr = h2[ds, :], gx[ds, :]
            a3 = nn(h2r, wc3).astype(BF16).astype(F32)
            u = nt(gr, wc4)
            h3, da = gelu_both(a3)
            h3 = h3.astype(BF16)
            da = (u * da).astype(BF16)
            pb[par, 0] += tn(h3, gr)
            pb[par, 1] += tn(h2r, da)
            prev = jnp.where(c == 0, gr.astype(F32), dh[ds, :])
            dh[ds, :] = prev + nt(da, wc3)

        @pl.when(c == NCH - 1)
        def _():
            h2[block(r), :] = dh[block(r), :].astype(BF16)
            x_copy(r).start()
        return carry

    def second_step(g, carry):
        i0 = g - NCH * NRB
        c, r = lax.div(i0, NRB), lax.rem(i0, NRB)
        par = lax.rem(c, 2)
        slot = lax.rem(i0, 2)

        @pl.when(i0 + 1 < NCH * NRB)
        def _():
            a_copy(i0 + 1).start()
        comm(g)

        @pl.when(c == 0)
        def _():
            x_copy(r).wait()

        @pl.when(r == 0)
        def _():
            pb[par] = jnp.zeros_like(pb[par])
        a_copy(i0).wait()

        wc2 = w2[pl.ds(al(c * ffc, ffc), ffc), :]
        for i in range(SUBS):
            ds = pl.ds(al(r * rows + i * sub, sub), sub)
            dr, xr = h2[ds, :], gx[ds, :]
            a1 = a1b[slot, i * sub : (i + 1) * sub, :].astype(F32)
            v = nt(dr, wc2)
            h1, da = gelu_both(a1)
            h1 = h1.astype(BF16)
            da = (v * da).astype(BF16)
            pb[par, 0] += tn(h1, dr)
            pb[par, 1] += tn(xr, da)
        return carry

    steps = NCH * NRB
    lax.fori_loop(0, steps, first_step, 0)
    w_copies[2].wait()
    lax.fori_loop(steps, 2 * steps, second_step, 0)

    def drain(g, carry):
        comm(g)
        return carry

    lax.fori_loop(2 * steps, 2 * steps + OFF["end"] + 1, drain, 0)


def solution(mesh):
    batch_spec = P(("z", "y", "xc"), None)
    whole_spec = P(None, None)
    any_spec = pl.BlockSpec(memory_space=pl.ANY)

    def device_step(x_loc, g_loc, w_one, w_two, w_three, w_four):
        n, d = x_loc.shape
        ff = w_one.shape[1]
        rows, ffc = n // NRB, ff // NCH
        mm = 2 * n * d * ff
        a1, h2 = pl.pallas_call(
            fwd_kernel,
            grid=(NRB,),
            in_specs=[
                pl.BlockSpec((rows, d), lambda i: (i, 0)),
                pl.BlockSpec((d, ff), lambda i: (0, 0)),
                pl.BlockSpec((ff, d), lambda i: (0, 0)),
            ],
            out_specs=[
                pl.BlockSpec((rows, ff), lambda i: (i, 0)),
                pl.BlockSpec((rows, d), lambda i: (i, 0)),
            ],
            out_shape=[jax.ShapeDtypeStruct((n, ff), BF16), jax.ShapeDtypeStruct((n, d), BF16)],
            compiler_params=pltpu.CompilerParams(vmem_limit_bytes=VMEM_LIMIT),
            cost_estimate=pl.CostEstimate(flops=2 * mm, bytes_accessed=2 * n * (ff + 2 * d), transcendentals=n * ff),
            name="fwd",
        )(x_loc, w_one, w_two)

        out = pl.pallas_call(
            grad_kernel,
            in_specs=[any_spec] * 7,
            out_specs=any_spec,
            out_shape=jax.ShapeDtypeStruct((UNITS, 2, d, ffc), F32),
            scratch_shapes=[
                pltpu.VMEM((n, d), BF16),
                pltpu.VMEM((n, d), BF16),
                pltpu.VMEM((n, d), F32),
                pltpu.VMEM((ff, d), BF16),
                pltpu.VMEM((d, ff), BF16),
                pltpu.VMEM((ff, d), BF16),
                pltpu.VMEM((2, rows, ffc), BF16),
                pltpu.VMEM((2, 2, d, ffc), F32),
                pltpu.VMEM((SLOTS, 2, d // 2, ffc), F32),
                pltpu.VMEM((SLOTS, 2, 2, d // 8, ffc), F32),
                pltpu.VMEM((SLOTS, 2, 2, d // 16, ffc), F32),
                pltpu.VMEM((SLOTS, 3, 2, 2, d // 64, ffc), F32),
                pltpu.SemaphoreType.DMA((3,)),
                pltpu.SemaphoreType.DMA((NRB,)),
                pltpu.SemaphoreType.DMA((NRB,)),
                pltpu.SemaphoreType.DMA((NRB,)),
                pltpu.SemaphoreType.DMA((2,)),
                pltpu.SemaphoreType.DMA((UNITS, 2)),
                pltpu.SemaphoreType.DMA((UNITS, 22)),
                pltpu.SemaphoreType.DMA((UNITS, 22)),
                pltpu.SemaphoreType.REGULAR((SLOTS,)),
            ],
            compiler_params=pltpu.CompilerParams(
                collective_id=0, has_side_effects=True, vmem_limit_bytes=VMEM_LIMIT
            ),
            cost_estimate=pl.CostEstimate(flops=8 * mm, bytes_accessed=2 * n * (ff + 3 * d), transcendentals=2 * n * ff),
            name="grads",
        )(x_loc, g_loc, h2, a1, w_two, w_three, w_four)

        def stack_rows(v):
            return v.reshape(ff, d)

        def stack_cols(v):
            return v.transpose(1, 0, 2).reshape(d, ff)

        return (
            stack_cols(out[NCH:, 1]),
            stack_rows(out[NCH:, 0]),
            stack_cols(out[:NCH, 1]),
            stack_rows(out[:NCH, 0]),
        )

    return jax.shard_map(
        device_step,
        mesh=mesh,
        in_specs=(batch_spec, batch_spec, whole_spec, whole_spec, whole_spec, whole_spec),
        out_specs=(whole_spec, whole_spec, whole_spec, whole_spec),
        check_vma=False,
    )
```

time: 880 us -> 367 us (0.42)
  waiting for transfers between devices: 490 us -> 0 us
  matrix products: 339 us -> 0 us
  Pallas kernels: 0 us -> 332 us
  local copies, waits for them, and re-layouts: 11.9 us -> 33.7 us
  other arithmetic: 19 us -> 0 us
  between operations: 14.5 us -> 0.64 us
    dot_general x10 -> x0, matrix products: 339 us -> none  [the longest x1 57.9 us: device_step(): jnp.einsum('nd,fd->nf', g_loc, w_four, preferred_element_type=jnp.float32)]
    pallas_call x0 -> x2, Pallas kernels: none -> 332 us  [the longest x1 282 us: device_step(): pl.pallas_call(grad_kernel, in_specs=[any_spec] * 7, out_specs=any_spec,...]
    all_gather x8 -> x0, waiting for transfers between devices: 213 us -> none  [the longest x4 129 us: reduce_grad(): reduced = lax.all_gather(reduced, 'xc', axis=0, tiled=True)]
    psum x1 -> x0, waiting for transfers between devices: 123 us -> none  [reduce_grad(): reduced = lax.psum(reduced, 'z')]
    reduce_scatter x6 -> x0, waiting for transfers between devices: 108 us -> none  [the longest x4 65.5 us: reduce_grad(): lax.psum_scatter(local_grad, 'xc', scatter_dimension=0, tiled=True)]
    unnamed x19 -> x0, waiting for transfers between devices: 44.9 us -> none
    div x4 -> x0, other arithmetic: 19 us -> none  [reduce_grad(): return reduced / n_dev]
    slice x0 -> x1, local copies, waits for them, and re-layouts: none -> 12.5 us  [device_step(): out[:NCH, 0]]
  transfers between devices with their start and end apart: 17 -> 0, of which waited for: 15 -> 0; matrix products, arithmetic and copies ran while one was open for 23% -> 0% of each run, Pallas kernels for 0% -> 0%
where the time goes in v1:
time: 367 us
  Pallas kernels  332 us (90%)
  local copies, waits for them, and re-layouts  33.7 us (9%)
    pallas_call x1, Pallas kernels, device_step(): pl.pallas_call(grad_kernel, in_specs=[any_spec] * 7, out_specs=any_spec,...  282 us
    pallas_call x1, Pallas kernels, device_step(): pl.pallas_call(fwd_kernel, grid=(NRB,), in_specs=[pl.BlockSpec((rows, d),...  50.3 us
    slice x1, local copies, waits for them, and re-layouts, device_step(): out[:NCH, 0]  12.5 us
    unnamed x2, local copies, waits for them, and re-layouts  10.7 us
    transpose x2, local copies, waits for them, and re-layouts, stack_cols(): return v.transpose(1, 0, 2).reshape(d, ff)  10.5 us

profile of v1, /device:TPU:0, one launch (start us, length us, event | category | flops | bytes accessed | tf_op | source)
XLA Modules:
  0.0 366.5 jit_solution(10290148966525038632)
XLA Ops:
  0.6 50.3 %fwd.1 = (bf16[8192,2048]{1,0:T(8,128)(2,1)}, bf16[8192,512]{1,0:T(8,128)(2,1)}) custom-call(bf16[8192,512]{1,0:T(8,128)(2,1)} %x_hbm.1, bf16[512,2048]{1,0:T(8,128)(2,1)} %w1_ref.1, bf16[2048,512]{1,0:T(8,128)(2,1)} %w2_hbm.1), custom_call_target="tpu_custom_call" | custom-call | flops 34359738368 | bytes 50331648 | tf_op jit(solution)/shard_map/fwd/pallas_call | solution.py:385
  51.0 281.9 %grads.1 = f32[8,2,512,512]{3,2,1,0:T(8,128)} custom-call(bf16[8192,512]{1,0:T(8,128)(2,1)} %x_hbm.1, bf16[8192,512]{1,0:T(8,128)(2,1)} %g_hbm.1, bf16[8192,512]{1,0:T(8,128)(2,1)} %get-tuple-element.6.h2_hbm, bf16[8192,2048]{1,0:T(8,128)(2,1)} %get-tuple-element.7.a1_hbm, bf16[2048,512]{1,0:T(8,128)(2,1)} %w2_hbm.1, bf16[512,2048]{1,0:T(8,128)(2,1)} %w3_hbm.1, ...), custom_call_target="tpu_custom_call" | custom-call | flops 137438953472 | bytes 58720256 | tf_op jit(solution)/shard_map/grads/pallas_call | solution.py:403
  332.9 12.5 %fusion = (f32[4,1,512,512]{3,2,1,0:T(8,128)}, f32[512,4,512]{2,0,1:T(8,128)}, f32[4,1,512,512]{3,2,1,0:T(8,128)}, f32[512,4,512]{2,0,1:T(8,128)}) fusion(f32[8,2,512,512]{3,2,1,0:T(8,128)} %grads.1), kind=kLoop, calls=%fused_computation.2 | loop fusion | bytes 33554432 | tf_op jit(solution)/shard_map/slice | solution.py:448
  345.4 5.2 %copy.11 = f32[512,4,512]{0,2,1:T(8,128)} copy(f32[512,4,512]{2,0,1:T(8,128)} %get-tuple-element.13) | data formatting | bytes 8388608 | tf_op jit(solution)/shard_map/transpose | solution.py:442
  350.6 5.3 %copy.13 = f32[512,2048]{1,0:T(8,128)} copy(f32[512,2048]{0,1:T(8,128)} %bitcast.12) | data formatting | bytes 8388608
  356.0 5.2 %copy.10 = f32[512,4,512]{0,2,1:T(8,128)} copy(f32[512,4,512]{2,0,1:T(8,128)} %get-tuple-element.15) | data formatting | bytes 8388608 | tf_op jit(solution)/shard_map/transpose | solution.py:442
  361.2 5.3 %copy.12 = f32[512,2048]{1,0:T(8,128)} copy(f32[512,2048]{0,1:T(8,128)} %bitcast.13) | data formatting | bytes 8388608

commit v2 on v1

--- a/solution.py
+++ b/solution.py
@@ -18,7 +18,8 @@
 NRB = 8
 UNITS = 2 * NCH
 SLOTS = 4
-SUBS = 2
+SUBS = 4
+EROWS = 16
 
 OFF = dict(d=0, s1=2, s2=6, z=9, zg=14, s2g=19, s1g=22, dg=26, end=29)
 
@@ -50,22 +51,70 @@
     return h, grad
 
 
-def fwd_kernel(x_ref, w1_ref, w2_ref, a1_ref, h2_ref):
+def woven(first, second):
+    order = [((i + 0.5) / len(first), 0, f) for i, f in enumerate(first)]
+    order += [((i + 0.5) / len(second), 1, f) for i, f in enumerate(second)]
+    for _, _, f in sorted(order, key=lambda e: e[:2]):
+        f()
+
+
+def pipelined(count, front, middle, back, back_first=True):
+    for f in front(0):
+        f()
+    for j in range(count):
+        around = [front(j + 1) if j + 1 < count else [], back(j - 1) if j else []]
+        around = around[1] + around[0] if back_first else around[0] + around[1]
+        woven(around, middle(j))
+    for f in back(count - 1):
+        f()
+
+
+def fwd_kernel(x_ref, w1_ref, w2_ref, a1_ref, h2_ref, hb, acc):
+    rows, d = x_ref.shape
     ffc = w1_ref.shape[1] // NCH
-    x = x_ref[...]
-    acc = x.astype(F32)
-    for c in range(NCH):
-        cols = slice(c * ffc, (c + 1) * ffc)
-        a1 = nn(x, w1_ref[:, cols]).astype(BF16)
-        a1_ref[:, cols] = a1
-        h1 = gelu_only(a1.astype(F32)).astype(BF16)
-        acc += nn(h1, w2_ref[cols, :])
-    h2_ref[...] = acc.astype(BF16)
+    half = rows // 2
+    er = min(EROWS, half)
+
+    def place(j):
+        c, n = j // 2, j % 2
+        return slice(c * ffc, (c + 1) * ffc), slice(n * half, (n + 1) * half), c
+
+    def front(j):
+        cols, at, c = place(j)
+
+        def up():
+            a1_ref[at, cols] = nn(x_ref[at, :], w1_ref[:, cols]).astype(BF16)
+
+        return [up]
+
+    def middle(j):
+        cols, at, c = place(j)
+
+        def piece(i):
+            ds = slice(at.start + i, at.start + i + er)
+            hb[ds, cols] = gelu_only(a1_ref[ds, cols].astype(F32)).astype(BF16)
+
+        return [functools.partial(piece, i) for i in range(0, half, er)]
+
+    def back(j):
+        cols, at, c = place(j)
+
+        def down():
+            prev = x_ref[at, :].astype(F32) if c == 0 else acc[at, :]
+            total = prev + nn(hb[at, cols], w2_ref[cols, :])
+            if c == NCH - 1:
+                h2_ref[at, :] = total.astype(BF16)
+            else:
+                acc[at, :] = total
+
+        return [down]
+
+    pipelined(2 * NCH, front, middle, back, back_first=False)
 
 
 def grad_kernel(
     x_hbm, g_hbm, h2_hbm, a1_hbm, w2_hbm, w3_hbm, w4_hbm, o_hbm,
-    h2, gx, dh, w2, w3, w4, a1b, pb, q, r1, r2, rz,
+    h2, gx, dh, w2, w3, w4, a1b, ab, ub, hb, db, pb, q, r1, r2, rz,
     wsem, hsem, gsem, xsem, asem, lsem, ssem, rsem, csem,
 ):
     d = h2.shape[1]
@@ -285,6 +334,7 @@
         stage(g, "s1", do_s1)
 
     sub = rows // SUBS
+    er = min(EROWS, sub)
 
     def first_step(g, carry):
         c, r = lax.div(g, NRB), lax.rem(g, NRB)
@@ -305,21 +355,49 @@
         def _():
             pb[par] = jnp.zeros_like(pb[par])
 
-        cols = pl.ds(al(c * ffc, ffc), ffc)
-        wc3 = w3[:, cols]
-        wc4 = w4[cols, :]
-        for i in range(SUBS):
-            ds = pl.ds(al(r * rows + i * sub, sub), sub)
-            h2r, gr = h2[ds, :], gx[ds, :]
-            a3 = nn(h2r, wc3).astype(BF16).astype(F32)
-            u = nt(gr, wc4)
-            h3, da = gelu_both(a3)
-            h3 = h3.astype(BF16)
-            da = (u * da).astype(BF16)
-            pb[par, 0] += tn(h3, gr)
-            pb[par, 1] += tn(h2r, da)
-            prev = jnp.where(c == 0, gr.astype(F32), dh[ds, :])
-            dh[ds, :] = prev + nt(da, wc3)
+        hf = ffc // 2
+
+        def rows_of(j):
+            return pl.ds(al(r * rows + j * sub, sub), sub), slice(j * sub, (j + 1) * sub)
+
+        def front(j):
+            ds, at = rows_of(j)
+
+            def act(n):
+                col = pl.ds(al(c * ffc + n * hf, hf), hf)
+                ab[at, n * hf : (n + 1) * hf] = nn(h2[ds, :], w3[:, col]).astype(BF16)
+
+            def up(n):
+                col = pl.ds(al(c * ffc + n * hf, hf), hf)
+                ub[at, n * hf : (n + 1) * hf] = nt(gx[ds, :], w4[col, :])
+
+            return [functools.partial(f, n) for n in range(2) for f in (act, up)]
+
+        def middle(j):
+            def piece(i):
+                at = slice(j * sub + i, j * sub + i + er)
+                h3, da = gelu_both(ab[at, :].astype(F32))
+                hb[at, :] = h3.astype(BF16)
+                db[at, :] = (ub[at, :] * da).astype(BF16)
+
+            return [functools.partial(piece, i) for i in range(0, sub, er)]
+
+        def back(j):
+            ds, at = rows_of(j)
+
+            def p4():
+                pb[par, 0] += tn(hb[at, :], gx[ds, :])
+
+            def p3():
+                pb[par, 1] += tn(h2[ds, :], db[at, :])
+
+            def down():
+                prev = jnp.where(c == 0, gx[ds, :].astype(F32), dh[ds, :])
+                dh[ds, :] = prev + nt(db[at, :], w3[:, pl.ds(al(c * ffc, ffc), ffc)])
+
+            return [p4, p3, down]
+
+        pipelined(SUBS, front, middle, back)
 
         @pl.when(c == NCH - 1)
         def _():
@@ -347,17 +425,38 @@
             pb[par] = jnp.zeros_like(pb[par])
         a_copy(i0).wait()
 
-        wc2 = w2[pl.ds(al(c * ffc, ffc), ffc), :]
-        for i in range(SUBS):
-            ds = pl.ds(al(r * rows + i * sub, sub), sub)
-            dr, xr = h2[ds, :], gx[ds, :]
-            a1 = a1b[slot, i * sub : (i + 1) * sub, :].astype(F32)
-            v = nt(dr, wc2)
-            h1, da = gelu_both(a1)
-            h1 = h1.astype(BF16)
-            da = (v * da).astype(BF16)
-            pb[par, 0] += tn(h1, dr)
-            pb[par, 1] += tn(xr, da)
+        def rows_of(j):
+            return pl.ds(al(r * rows + j * sub, sub), sub), slice(j * sub, (j + 1) * sub)
+
+        def front(j):
+            ds, at = rows_of(j)
+
+            def up():
+                ub[at, :] = nt(h2[ds, :], w2[pl.ds(al(c * ffc, ffc), ffc), :])
+
+            return [up]
+
+        def middle(j):
+            def piece(i):
+                at = slice(j * sub + i, j * sub + i + er)
+                h1, da = gelu_both(a1b[slot, at, :].astype(F32))
+                hb[at, :] = h1.astype(BF16)
+                db[at, :] = (ub[at, :] * da).astype(BF16)
+
+            return [functools.partial(piece, i) for i in range(0, sub, er)]
+
+        def back(j):
+            ds, at = rows_of(j)
+
+            def p2():
+                pb[par, 0] += tn(hb[at, :], h2[ds, :])
+
+            def p1():
+                pb[par, 1] += tn(gx[ds, :], db[at, :])
+
+            return [p2, p1]
+
+        pipelined(SUBS, front, middle, back)
         return carry
 
     steps = NCH * NRB
@@ -370,6 +469,25 @@
         return carry
 
     lax.fori_loop(2 * steps, 2 * steps + OFF["end"] + 1, drain, 0)
+
+
+def finish_kernel(o_hbm, d1, d2, d3, d4, buf, isem, osem):
+    half = UNITS // 2
+    d, ffc = buf.shape[2], buf.shape[3]
+    loads = [pltpu.make_async_copy(o_hbm.at[k], buf.at[k], isem.at[k]) for k in range(UNITS)]
+    for copy in loads:
+        copy.start()
+    stores = []
+    for k in range(UNITS):
+        loads[k].wait()
+        tall, wide = (d4, d3) if k < half else (d2, d1)
+        at = pl.ds((k % half) * ffc, ffc)
+        stores.append(pltpu.make_async_copy(buf.at[k, 0], tall.at[at, :], osem.at[k, 0]))
+        stores.append(pltpu.make_async_copy(buf.at[k, 1], wide.at[:, at], osem.at[k, 1]))
+        stores[-2].start()
+        stores[-1].start()
+    for copy in stores:
+        copy.wait()
 
 
 def solution(mesh):
@@ -395,6 +513,7 @@
                 pl.BlockSpec((rows, d), lambda i: (i, 0)),
             ],
             out_shape=[jax.ShapeDtypeStruct((n, ff), BF16), jax.ShapeDtypeStruct((n, d), BF16)],
+            scratch_shapes=[pltpu.VMEM((rows, ff), BF16), pltpu.VMEM((rows, d), F32)],
             compiler_params=pltpu.CompilerParams(vmem_limit_bytes=VMEM_LIMIT),
             cost_estimate=pl.CostEstimate(flops=2 * mm, bytes_accessed=2 * n * (ff + 2 * d), transcendentals=n * ff),
             name="fwd",
@@ -413,6 +532,10 @@
                 pltpu.VMEM((d, ff), BF16),
                 pltpu.VMEM((ff, d), BF16),
                 pltpu.VMEM((2, rows, ffc), BF16),
+                pltpu.VMEM((rows, ffc), BF16),
+                pltpu.VMEM((rows, ffc), F32),
+                pltpu.VMEM((rows, ffc), BF16),
+                pltpu.VMEM((rows, ffc), BF16),
                 pltpu.VMEM((2, 2, d, ffc), F32),
                 pltpu.VMEM((SLOTS, 2, d // 2, ffc), F32),
                 pltpu.VMEM((SLOTS, 2, 2, d // 8, ffc), F32),
@@ -435,18 +558,20 @@
             name="grads",
         )(x_loc, g_loc, h2, a1, w_two, w_three, w_four)
 
-        def stack_rows(v):
-            return v.reshape(ff, d)
-
-        def stack_cols(v):
-            return v.transpose(1, 0, 2).reshape(d, ff)
-
-        return (
-            stack_cols(out[NCH:, 1]),
-            stack_rows(out[NCH:, 0]),
-            stack_cols(out[:NCH, 1]),
-            stack_rows(out[:NCH, 0]),
-        )
+        wide, tall = jax.ShapeDtypeStruct((d, ff), F32), jax.ShapeDtypeStruct((ff, d), F32)
+        return pl.pallas_call(
+            finish_kernel,
+            in_specs=[any_spec],
+            out_specs=[any_spec] * 4,
+            out_shape=[wide, tall, wide, tall],
+            scratch_shapes=[
+                pltpu.VMEM((UNITS, 2, d, ffc), F32),
+                pltpu.SemaphoreType.DMA((UNITS,)),
+                pltpu.SemaphoreType.DMA((UNITS, 2)),
+            ],
+            compiler_params=pltpu.CompilerParams(vmem_limit_bytes=VMEM_LIMIT),
+            name="finish",
+        )(out)
 
     return jax.shard_map(
         device_step,

time: 367 us -> 319 us (0.87)
  local copies, waits for them, and re-layouts: 33.7 us -> 0 us
  Pallas kernels: 332 us -> 318 us
    pallas_call x1, Pallas kernels: 282 us -> 265 us  [device_step(): pl.pallas_call(grad_kernel, in_specs=[any_spec] * 7, out_specs=any_spec,...]
    slice x1 -> x0, local copies, waits for them, and re-layouts: 12.5 us -> none  [device_step(): out[:NCH, 0]]
    pallas_call x0 -> x1, Pallas kernels: none -> 11.9 us  [device_step(): pl.pallas_call(finish_kernel, in_specs=[any_spec], out_specs=[any_spec] *...]
    unnamed x2 -> x0, local copies, waits for them, and re-layouts: 10.7 us -> none
    transpose x2 -> x0, local copies, waits for them, and re-layouts: 10.5 us -> none  [stack_cols(): return v.transpose(1, 0, 2).reshape(d, ff)]
    pallas_call x1, Pallas kernels: 50.3 us -> 41.9 us  [device_step(): pl.pallas_call(fwd_kernel, grid=(NRB,), in_specs=[pl.BlockSpec((rows, d),...]
where the time goes in v2:
time: 319 us
  Pallas kernels  318 us (100%)
    pallas_call x1, Pallas kernels, device_step(): pl.pallas_call(grad_kernel, in_specs=[any_spec] * 7, out_specs=any_spec,...  265 us
    pallas_call x1, Pallas kernels, device_step(): pl.pallas_call(fwd_kernel, grid=(NRB,), in_specs=[pl.BlockSpec((rows, d),...  41.9 us
    pallas_call x1, Pallas kernels, device_step(): pl.pallas_call(finish_kernel, in_specs=[any_spec], out_specs=[any_spec] *...  11.9 us

profile of v2, /device:TPU:0, one launch (start us, length us, event | category | flops | bytes accessed | tf_op | source)
XLA Modules:
  0.0 319.0 jit_solution(8034106420733640488)
XLA Ops:
  0.6 41.9 %fwd.1 = (bf16[8192,2048]{1,0:T(8,128)(2,1)}, bf16[8192,512]{1,0:T(8,128)(2,1)}) custom-call(bf16[8192,512]{1,0:T(8,128)(2,1)} %x_hbm.1, bf16[512,2048]{1,0:T(8,128)(2,1)} %w1_ref.1, bf16[2048,512]{1,0:T(8,128)(2,1)} %w2_hbm.1), custom_call_target="tpu_custom_call" | custom-call | flops 34359738368 | bytes 50331648 | tf_op jit(solution)/shard_map/fwd/pallas_call | solution.py:503
  42.5 264.6 %grads.1.o_hbm = f32[8,2,512,512]{3,2,1,0:T(8,128)} custom-call(bf16[8192,512]{1,0:T(8,128)(2,1)} %x_hbm.1, bf16[8192,512]{1,0:T(8,128)(2,1)} %g_hbm.1, bf16[8192,512]{1,0:T(8,128)(2,1)} %get-tuple-element.6.h2_hbm, bf16[8192,2048]{1,0:T(8,128)(2,1)} %get-tuple-element.7.a1_hbm, bf16[2048,512]{1,0:T(8,128)(2,1)} %w2_hbm.1, bf16[512,2048]{1,0:T(8,128)(2,1)} %w3_hbm.1, ...), custom_call_target="tpu_custom_call" | custom-call | flops 137438953472 | bytes 58720256 | tf_op jit(solution)/shard_map/grads/pallas_call | solution.py:522
  307.1 11.9 %finish.1 = (f32[512,2048]{1,0:T(8,128)}, f32[2048,512]{1,0:T(8,128)}, f32[512,2048]{1,0:T(8,128)}, f32[2048,512]{1,0:T(8,128)}) custom-call(f32[8,2,512,512]{3,2,1,0:T(8,128)} %grads.1.o_hbm), custom_call_target="tpu_custom_call" | custom-call | tf_op jit(solution)/shard_map/finish/pallas_call | solution.py:562

commit v3 on v2

--- a/solution.py
+++ b/solution.py
@@ -14,14 +14,16 @@
 MESH = pl.DeviceIdType.MESH
 VMEM_LIMIT = 67_000_000
 
-NCH = 4
-NRB = 8
+NCF = 4
+NRF = 8
+NCH = 8
+NRB = 4
 UNITS = 2 * NCH
-SLOTS = 4
+SLOTS = 8
 SUBS = 4
 EROWS = 16
 
-OFF = dict(d=0, s1=2, s2=6, z=9, zg=14, s2g=19, s1g=22, dg=26, end=29)
+OFF = dict(d=0, s1=2, s2=5, z=8, zg=12, s2g=16, s1g=19, dg=22, end=25)
 
 
 def nn(a, b):
@@ -71,7 +73,7 @@
 
 def fwd_kernel(x_ref, w1_ref, w2_ref, a1_ref, h2_ref, hb, acc):
     rows, d = x_ref.shape
-    ffc = w1_ref.shape[1] // NCH
+    ffc = w1_ref.shape[1] // NCF
     half = rows // 2
     er = min(EROWS, half)
 
@@ -102,14 +104,14 @@
         def down():
             prev = x_ref[at, :].astype(F32) if c == 0 else acc[at, :]
             total = prev + nn(hb[at, cols], w2_ref[cols, :])
-            if c == NCH - 1:
+            if c == NCF - 1:
                 h2_ref[at, :] = total.astype(BF16)
             else:
                 acc[at, :] = total
 
         return [down]
 
-    pipelined(2 * NCH, front, middle, back, back_first=False)
+    pipelined(2 * NCF, front, middle, back, back_first=False)
 
 
 def grad_kernel(
@@ -120,7 +122,8 @@
     d = h2.shape[1]
     rows = h2.shape[0] // NRB
     ffc = w3.shape[1] // NCH
-    half, col, s1n, s2n, zn = d // 2, d // 4, d // 8, d // 16, d // 64
+    half, col, s1n, s2n = ffc // 2, ffc // 4, ffc // 8, ffc // 16
+    hd = d // 2
 
     xc, y, z = lax.axis_index("xc"), lax.axis_index("y"), lax.axis_index("z")
     x, core = lax.div(xc, 2), lax.rem(xc, 2)
@@ -177,7 +180,7 @@
 
     def remote(src, dst, k, i, peer):
         return pltpu.make_async_remote_copy(
-            src_ref=src, dst_ref=dst, send_sem=ssem.at[k, i], recv_sem=rsem.at[k, i],
+            src_ref=src, dst_ref=dst, send_sem=ssem.at[lax.rem(k, SLOTS), i], recv_sem=rsem.at[lax.rem(k, SLOTS), i],
             device_id=peer, device_id_type=MESH,
         )
 
@@ -187,10 +190,10 @@
             q.at[lax.rem(k, SLOTS)], k, 0, to_core)]
 
     def q_at(k, start, size):
-        return q.at[lax.rem(k, SLOTS), :, pl.ds(al(start, zn), size), :]
+        return q.at[lax.rem(k, SLOTS), :, pl.ds(al(start, s2n), size), :]
 
     def o_at(k, start, size):
-        return o_hbm.at[k, :, pl.ds(al(core * half + start, zn), size), :]
+        return o_hbm.at[k, :, pl.ds(al(core * half + start, s2n), size), :]
 
     def c_s1(k):
         sl = lax.rem(k, SLOTS)
@@ -206,26 +209,31 @@
             remote(q_at(k, yb + (1 - x) * s2n, s2n), r2.at[sl, 1], k, 4, to_x),
         ]
 
+    def z_piece(k, block, base):
+        return q.at[lax.rem(k, SLOTS), block, pl.ds(al(base, s2n), s2n), :]
+
+    def o_piece(k, base):
+        return o_hbm.at[k, z, pl.ds(al(core * half + base, s2n), s2n), :]
+
     def c_z(k):
         sl = lax.rem(k, SLOTS)
         out = []
         for j in range(3):
-            zz = lax.rem(z + j + 1, 4) * zn
-            out.append(remote(q_at(k, xya + zz, zn), rz.at[sl, j, 0], k, 5 + 2 * j, to_z[j]))
-            out.append(remote(q_at(k, yxb + zz, zn), rz.at[sl, j, 1], k, 6 + 2 * j, to_z[j]))
+            zz = lax.rem(z + j + 1, 4)
+            for n, base in enumerate((xya, yxb)):
+                out.append(remote(z_piece(k, zz, base), rz.at[sl, j, n], k, 5 + 2 * j + n, to_z[j]))
         return out
 
     def c_zg(k):
         out = []
         for j in range(3):
             for n, base in enumerate((xya, yxb)):
-                at = base + z * zn
-                out.append(remote(q_at(k, at, zn), o_at(k, at, zn), k, 11 + 2 * j + n, to_z[j]))
+                out.append(remote(z_piece(k, z, base), o_piece(k, base), k, 11 + 2 * j + n, to_z[j]))
         return out
 
     def c_local(k):
         return [
-            pltpu.make_async_copy(q_at(k, base + z * zn, zn), o_at(k, base + z * zn, zn), lsem.at[k, n])
+            pltpu.make_async_copy(z_piece(k, z, base), o_piece(k, base), lsem.at[lax.rem(k, SLOTS), n])
             for n, base in enumerate((xya, yxb))
         ]
 
@@ -254,7 +262,7 @@
 
     def q_add(k, at, size, value):
         sl = lax.rem(k, SLOTS)
-        ds = pl.ds(al(at, zn), size)
+        ds = pl.ds(al(at, s2n), size)
         q[sl, :, ds, :] = q[sl, :, ds, :] + value
 
     def stage(g, name, action):
@@ -295,9 +303,9 @@
         wait(c_z(k))
         sl = lax.rem(k, SLOTS)
         for n, base in enumerate((xya, yxb)):
-            ds = pl.ds(al(base + z * zn, zn), zn)
-            total = (q[sl, :, ds, :] + rz[sl, 0, n]) + (rz[sl, 1, n] + rz[sl, 2, n])
-            q[sl, :, ds, :] = total * (1.0 / 32.0)
+            ds = pl.ds(al(base, s2n), s2n)
+            total = (q[sl, z, ds, :] + rz[sl, 0, n]) + (rz[sl, 1, n] + rz[sl, 2, n])
+            q[sl, z, ds, :] = total * (1.0 / 32.0)
         start(c_zg(k))
         start(c_local(k))
 
@@ -335,6 +343,7 @@
 
     sub = rows // SUBS
     er = min(EROWS, sub)
+    sub2 = sub // 2
 
     def first_step(g, carry):
         c, r = lax.div(g, NRB), lax.rem(g, NRB)
@@ -355,21 +364,20 @@
         def _():
             pb[par] = jnp.zeros_like(pb[par])
 
-        hf = ffc // 2
+        cols = pl.ds(al(c * ffc, ffc), ffc)
+        hs = sub // 2
 
         def rows_of(j):
             return pl.ds(al(r * rows + j * sub, sub), sub), slice(j * sub, (j + 1) * sub)
 
         def front(j):
-            ds, at = rows_of(j)
-
             def act(n):
-                col = pl.ds(al(c * ffc + n * hf, hf), hf)
-                ab[at, n * hf : (n + 1) * hf] = nn(h2[ds, :], w3[:, col]).astype(BF16)
+                ds, at = pl.ds(al(r * rows + j * sub + n * hs, hs), hs), slice(j * sub + n * hs, j * sub + (n + 1) * hs)
+                ab[at, :] = nn(h2[ds, :], w3[:, cols]).astype(BF16)
 
             def up(n):
-                col = pl.ds(al(c * ffc + n * hf, hf), hf)
-                ub[at, n * hf : (n + 1) * hf] = nt(gx[ds, :], w4[col, :])
+                ds, at = pl.ds(al(r * rows + j * sub + n * hs, hs), hs), slice(j * sub + n * hs, j * sub + (n + 1) * hs)
+                ub[at, :] = nt(gx[ds, :], w4[cols, :])
 
             return [functools.partial(f, n) for n in range(2) for f in (act, up)]
 
@@ -386,14 +394,18 @@
             ds, at = rows_of(j)
 
             def p4():
-                pb[par, 0] += tn(hb[at, :], gx[ds, :])
+                part = tn(hb[at, :], gx[ds, :])
+                pb[par, 0] += part[:, :hd]
+                pb[par, 1] += part[:, hd:]
 
             def p3():
-                pb[par, 1] += tn(h2[ds, :], db[at, :])
+                part = tn(h2[ds, :], db[at, :])
+                pb[par, 2] += part[:hd]
+                pb[par, 3] += part[hd:]
 
             def down():
                 prev = jnp.where(c == 0, gx[ds, :].astype(F32), dh[ds, :])
-                dh[ds, :] = prev + nt(db[at, :], w3[:, pl.ds(al(c * ffc, ffc), ffc)])
+                dh[ds, :] = prev + nt(db[at, :], w3[:, cols])
 
             return [p4, p3, down]
 
@@ -426,7 +438,7 @@
         a_copy(i0).wait()
 
         def rows_of(j):
-            return pl.ds(al(r * rows + j * sub, sub), sub), slice(j * sub, (j + 1) * sub)
+            return pl.ds(al(r * rows + j * sub2, sub2), sub2), slice(j * sub2, (j + 1) * sub2)
 
         def front(j):
             ds, at = rows_of(j)
@@ -438,25 +450,29 @@
 
         def middle(j):
             def piece(i):
-                at = slice(j * sub + i, j * sub + i + er)
+                at = slice(j * sub2 + i, j * sub2 + i + er)
                 h1, da = gelu_both(a1b[slot, at, :].astype(F32))
                 hb[at, :] = h1.astype(BF16)
                 db[at, :] = (ub[at, :] * da).astype(BF16)
 
-            return [functools.partial(piece, i) for i in range(0, sub, er)]
+            return [functools.partial(piece, i) for i in range(0, sub2, er)]
 
         def back(j):
             ds, at = rows_of(j)
 
             def p2():
-                pb[par, 0] += tn(hb[at, :], h2[ds, :])
+                part = tn(hb[at, :], h2[ds, :])
+                pb[par, 0] += part[:, :hd]
+                pb[par, 1] += part[:, hd:]
 
             def p1():
-                pb[par, 1] += tn(gx[ds, :], db[at, :])
+                part = tn(gx[ds, :], db[at, :])
+                pb[par, 2] += part[:hd]
+                pb[par, 3] += part[hd:]
 
             return [p2, p1]
 
-        pipelined(SUBS, front, middle, back)
+        pipelined(2 * SUBS, front, middle, back, back_first=False)
         return carry
 
     steps = NCH * NRB
@@ -473,7 +489,7 @@
 
 def finish_kernel(o_hbm, d1, d2, d3, d4, buf, isem, osem):
     half = UNITS // 2
-    d, ffc = buf.shape[2], buf.shape[3]
+    ffc, hd = buf.shape[2], buf.shape[3]
     loads = [pltpu.make_async_copy(o_hbm.at[k], buf.at[k], isem.at[k]) for k in range(UNITS)]
     for copy in loads:
         copy.start()
@@ -482,10 +498,12 @@
         loads[k].wait()
         tall, wide = (d4, d3) if k < half else (d2, d1)
         at = pl.ds((k % half) * ffc, ffc)
-        stores.append(pltpu.make_async_copy(buf.at[k, 0], tall.at[at, :], osem.at[k, 0]))
-        stores.append(pltpu.make_async_copy(buf.at[k, 1], wide.at[:, at], osem.at[k, 1]))
-        stores[-2].start()
-        stores[-1].start()
+        for n in range(2):
+            side = pl.ds(n * hd, hd)
+            stores.append(pltpu.make_async_copy(buf.at[k, n], tall.at[at, side], osem.at[k, n]))
+            stores.append(pltpu.make_async_copy(buf.at[k, 2 + n], wide.at[side, at], osem.at[k, 2 + n]))
+            stores[-2].start()
+            stores[-1].start()
     for copy in stores:
         copy.wait()
 
@@ -498,22 +516,22 @@
     def device_step(x_loc, g_loc, w_one, w_two, w_three, w_four):
         n, d = x_loc.shape
         ff = w_one.shape[1]
-        rows, ffc = n // NRB, ff // NCH
+        rows, ffc, frows = n // NRB, ff // NCH, n // NRF
         mm = 2 * n * d * ff
         a1, h2 = pl.pallas_call(
             fwd_kernel,
-            grid=(NRB,),
+            grid=(NRF,),
             in_specs=[
-                pl.BlockSpec((rows, d), lambda i: (i, 0)),
+                pl.BlockSpec((frows, d), lambda i: (i, 0)),
                 pl.BlockSpec((d, ff), lambda i: (0, 0)),
                 pl.BlockSpec((ff, d), lambda i: (0, 0)),
             ],
             out_specs=[
-                pl.BlockSpec((rows, ff), lambda i: (i, 0)),
-                pl.BlockSpec((rows, d), lambda i: (i, 0)),
+                pl.BlockSpec((frows, ff), lambda i: (i, 0)),
+                pl.BlockSpec((frows, d), lambda i: (i, 0)),
             ],
             out_shape=[jax.ShapeDtypeStruct((n, ff), BF16), jax.ShapeDtypeStruct((n, d), BF16)],
-            scratch_shapes=[pltpu.VMEM((rows, ff), BF16), pltpu.VMEM((rows, d), F32)],
+            scratch_shapes=[pltpu.VMEM((frows, ff), BF16), pltpu.VMEM((frows, d), F32)],
             compiler_params=pltpu.CompilerParams(vmem_limit_bytes=VMEM_LIMIT),
             cost_estimate=pl.CostEstimate(flops=2 * mm, bytes_accessed=2 * n * (ff + 2 * d), transcendentals=n * ff),
             name="fwd",
@@ -523,7 +541,7 @@
             grad_kernel,
             in_specs=[any_spec] * 7,
             out_specs=any_spec,
-            out_shape=jax.ShapeDtypeStruct((UNITS, 2, d, ffc), F32),
+            out_shape=jax.ShapeDtypeStruct((UNITS, 4, ffc, d // 2), F32),
             scratch_shapes=[
                 pltpu.VMEM((n, d), BF16),
                 pltpu.VMEM((n, d), BF16),
@@ -536,19 +554,19 @@
                 pltpu.VMEM((rows, ffc), F32),
                 pltpu.VMEM((rows, ffc), BF16),
                 pltpu.VMEM((rows, ffc), BF16),
-                pltpu.VMEM((2, 2, d, ffc), F32),
-                pltpu.VMEM((SLOTS, 2, d // 2, ffc), F32),
-                pltpu.VMEM((SLOTS, 2, 2, d // 8, ffc), F32),
-                pltpu.VMEM((SLOTS, 2, 2, d // 16, ffc), F32),
-                pltpu.VMEM((SLOTS, 3, 2, 2, d // 64, ffc), F32),
+                pltpu.VMEM((2, 4, ffc, d // 2), F32),
+                pltpu.VMEM((SLOTS, 4, ffc // 2, d // 2), F32),
+                pltpu.VMEM((SLOTS, 2, 4, ffc // 8, d // 2), F32),
+                pltpu.VMEM((SLOTS, 2, 4, ffc // 16, d // 2), F32),
+                pltpu.VMEM((SLOTS, 3, 2, ffc // 16, d // 2), F32),
                 pltpu.SemaphoreType.DMA((3,)),
                 pltpu.SemaphoreType.DMA((NRB,)),
                 pltpu.SemaphoreType.DMA((NRB,)),
                 pltpu.SemaphoreType.DMA((NRB,)),
                 pltpu.SemaphoreType.DMA((2,)),
-                pltpu.SemaphoreType.DMA((UNITS, 2)),
-                pltpu.SemaphoreType.DMA((UNITS, 22)),
-                pltpu.SemaphoreType.DMA((UNITS, 22)),
+                pltpu.SemaphoreType.DMA((SLOTS, 2)),
+                pltpu.SemaphoreType.DMA((SLOTS, 22)),
+                pltpu.SemaphoreType.DMA((SLOTS, 22)),
                 pltpu.SemaphoreType.REGULAR((SLOTS,)),
             ],
             compiler_params=pltpu.CompilerParams(
@@ -565,9 +583,9 @@
             out_specs=[any_spec] * 4,
             out_shape=[wide, tall, wide, tall],
             scratch_shapes=[
-                pltpu.VMEM((UNITS, 2, d, ffc), F32),
+                pltpu.VMEM((UNITS, 4, ffc, d // 2), F32),
                 pltpu.SemaphoreType.DMA((UNITS,)),
-                pltpu.SemaphoreType.DMA((UNITS, 2)),
+                pltpu.SemaphoreType.DMA((UNITS, 4)),
             ],
             compiler_params=pltpu.CompilerParams(vmem_limit_bytes=VMEM_LIMIT),
             name="finish",

time: 319 us -> 301 us (0.944)
  Pallas kernels: 318 us -> 300 us
    pallas_call x1, Pallas kernels: 265 us -> 246 us  [device_step(): pl.pallas_call(grad_kernel, in_specs=[any_spec] * 7, out_specs=any_spec,...]
where the time goes in v3:
time: 301 us
  Pallas kernels  300 us (100%)
    pallas_call x1, Pallas kernels, device_step(): pl.pallas_call(grad_kernel, in_specs=[any_spec] * 7, out_specs=any_spec,...  246 us
    pallas_call x1, Pallas kernels, device_step(): pl.pallas_call(fwd_kernel, grid=(NRF,), in_specs=[pl.BlockSpec((frows, d)...  41.9 us
    pallas_call x1, Pallas kernels, device_step(): pl.pallas_call(finish_kernel, in_specs=[any_spec], out_specs=[any_spec] *...  12.4 us

profile of v3, /device:TPU:0, one launch (start us, length us, event | category | flops | bytes accessed | tf_op | source)
XLA Modules:
  0.0 301.0 jit_solution(8270753231515813885)
XLA Ops:
  0.6 41.9 %fwd.1 = (bf16[8192,2048]{1,0:T(8,128)(2,1)}, bf16[8192,512]{1,0:T(8,128)(2,1)}) custom-call(bf16[8192,512]{1,0:T(8,128)(2,1)} %x_hbm.1, bf16[512,2048]{1,0:T(8,128)(2,1)} %w1_ref.1, bf16[2048,512]{1,0:T(8,128)(2,1)} %w2_hbm.1), custom_call_target="tpu_custom_call" | custom-call | flops 34359738368 | bytes 50331648 | tf_op jit(solution)/shard_map/fwd/pallas_call | solution.py:521
  42.5 246.1 %grads.1.o_hbm = f32[16,4,256,256]{3,2,1,0:T(8,128)} custom-call(bf16[8192,512]{1,0:T(8,128)(2,1)} %x_hbm.1, bf16[8192,512]{1,0:T(8,128)(2,1)} %g_hbm.1, bf16[8192,512]{1,0:T(8,128)(2,1)} %get-tuple-element.6.h2_hbm, bf16[8192,2048]{1,0:T(8,128)(2,1)} %get-tuple-element.7.a1_hbm, bf16[2048,512]{1,0:T(8,128)(2,1)} %w2_hbm.1, bf16[512,2048]{1,0:T(8,128)(2,1)} %w3_hbm.1, ...), custom_call_target="tpu_custom_call" | custom-call | flops 137438953472 | bytes 58720256 | tf_op jit(solution)/shard_map/grads/pallas_call | solution.py:540
  288.6 12.4 %finish.1 = (f32[512,2048]{1,0:T(8,128)}, f32[2048,512]{1,0:T(8,128)}, f32[512,2048]{1,0:T(8,128)}, f32[2048,512]{1,0:T(8,128)}) custom-call(f32[16,4,256,256]{3,2,1,0:T(8,128)} %grads.1.o_hbm), custom_call_target="tpu_custom_call" | custom-call | tf_op jit(solution)/shard_map/finish/pallas_call | solution.py:580

commit v4 on v3

--- a/solution.py
+++ b/solution.py
@@ -23,7 +23,11 @@
 SUBS = 4
 EROWS = 16
 
-OFF = dict(d=0, s1=2, s2=5, z=8, zg=12, s2g=16, s1g=19, dg=22, end=25)
+OFF = dict(
+    d=(0, 0), s1=(1, 2), s2=(3, 5), z=(5, 8), zg=(8, 11), s2g=(11, 15), s1g=(13, 18), dg=(15, 21), end=(17, 24)
+)
+EARLY = 6
+LAST = OFF["end"][1]
 
 
 def nn(a, b):
@@ -266,10 +270,14 @@
         q[sl, :, ds, :] = q[sl, :, ds, :] + value
 
     def stage(g, name, action):
-        t = g - OFF[name] - NRB
-        k = lax.div(t, NRB)
-
-        @pl.when((t >= 0) & (lax.rem(t, NRB) == 0) & (k < UNITS))
+        early, late = OFF[name]
+        te, tl = g - early - NRB, g - late - NRB
+        ke, kl = lax.div(te, NRB), lax.div(tl, NRB)
+        is_e = (te >= 0) & (lax.rem(te, NRB) == 0) & (ke < EARLY)
+        is_l = (tl >= 0) & (lax.rem(tl, NRB) == 0) & (kl >= EARLY) & (kl < UNITS)
+        k = jnp.where(is_e, ke, kl)
+
+        @pl.when(is_e | is_l)
         def _():
             action(k)
 
@@ -407,7 +415,7 @@
                 prev = jnp.where(c == 0, gx[ds, :].astype(F32), dh[ds, :])
                 dh[ds, :] = prev + nt(db[at, :], w3[:, cols])
 
-            return [p4, p3, down]
+            return [p3, p4, down]
 
         pipelined(SUBS, front, middle, back)
 
@@ -484,7 +492,7 @@
         comm(g)
         return carry
 
-    lax.fori_loop(2 * steps, 2 * steps + OFF["end"] + 1, drain, 0)
+    lax.fori_loop(2 * steps, 2 * steps + LAST + 1, drain, 0)
 
 
 def finish_kernel(o_hbm, d1, d2, d3, d4, buf, isem, osem):

time: 301 us -> 301 us (level)
  no operation moved by 1% of the time
where the time goes in v4:
time: 301 us
  Pallas kernels  301 us (100%)
    pallas_call x1, Pallas kernels, device_step(): pl.pallas_call(grad_kernel, in_specs=[any_spec] * 7, out_specs=any_spec,...  246 us
    pallas_call x1, Pallas kernels, device_step(): pl.pallas_call(fwd_kernel, grid=(NRF,), in_specs=[pl.BlockSpec((frows, d)...  41.9 us
    pallas_call x1, Pallas kernels, device_step(): pl.pallas_call(finish_kernel, in_specs=[any_spec], out_specs=[any_spec] *...  12.4 us

profile of v4, /device:TPU:0, one launch (start us, length us, event | category | flops | bytes accessed | tf_op | source)
XLA Modules:
  0.0 301.2 jit_solution(7619792949253348147)
XLA Ops:
  0.6 41.9 %fwd.1 = (bf16[8192,2048]{1,0:T(8,128)(2,1)}, bf16[8192,512]{1,0:T(8,128)(2,1)}) custom-call(bf16[8192,512]{1,0:T(8,128)(2,1)} %x_hbm.1, bf16[512,2048]{1,0:T(8,128)(2,1)} %w1_ref.1, bf16[2048,512]{1,0:T(8,128)(2,1)} %w2_hbm.1), custom_call_target="tpu_custom_call" | custom-call | flops 34359738368 | bytes 50331648 | tf_op jit(solution)/shard_map/fwd/pallas_call | solution.py:529
  42.5 246.3 %grads.1.o_hbm = f32[16,4,256,256]{3,2,1,0:T(8,128)} custom-call(bf16[8192,512]{1,0:T(8,128)(2,1)} %x_hbm.1, bf16[8192,512]{1,0:T(8,128)(2,1)} %g_hbm.1, bf16[8192,512]{1,0:T(8,128)(2,1)} %get-tuple-element.6.h2_hbm, bf16[8192,2048]{1,0:T(8,128)(2,1)} %get-tuple-element.7.a1_hbm, bf16[2048,512]{1,0:T(8,128)(2,1)} %w2_hbm.1, bf16[512,2048]{1,0:T(8,128)(2,1)} %w3_hbm.1, ...), custom_call_target="tpu_custom_call" | custom-call | flops 137438953472 | bytes 58720256 | tf_op jit(solution)/shard_map/grads/pallas_call | solution.py:548
  288.8 12.4 %finish.1 = (f32[512,2048]{1,0:T(8,128)}, f32[2048,512]{1,0:T(8,128)}, f32[512,2048]{1,0:T(8,128)}, f32[2048,512]{1,0:T(8,128)}) custom-call(f32[16,4,256,256]{3,2,1,0:T(8,128)} %grads.1.o_hbm), custom_call_target="tpu_custom_call" | custom-call | tf_op jit(solution)/shard_map/finish/pallas_call | solution.py:588
